TPU v7x, 32 devices: a whole 2x2x4 slice. The times are simulated.
32 devices in a mesh: groups: 2 (over y), fibre: 4 (over z), seg: 2 (over x), rec: 2 (over core).
Axes of the slice: x: 2, y: 2, z: 4, core: 2. Of those that a mesh axis runs over, the one named last changes fastest.
Arguments:
- records: bfloat16 [2, 2048, 1024], P('rec', 'fibre', ('groups', 'seg')), parts along dimension 2, may hold values from -6 to 6
- pairs: int32 [16, 2], replicated, may hold values from 0 to 15
- observed: float32 [32, 32, 256], P(('groups', 'fibre', 'seg')), parts along dimension 0, may hold values from -6 to 6
- lag_mask: int32 [32, 256], P(('groups', 'fibre', 'seg')), parts along dimension 0, may hold values 0 or 1
Outputs:
- adjoint_sources: bfloat16 [2, 2048, 1024], P('rec', 'fibre', ('groups', 'seg')), parts along dimension 2
There are 2 independent parts, one for each index of `groups`. A program takes and returns all parts, laid end to end along the dimension named above; an argument that names none is the same for every part. Nothing has to cross between parts.
All inputs are finite; a program needn't handle non-finite values. No bound on the sum of `lag_mask` on one device may be relied on, other than what follows from the above.
Results may differ from a plain program's by a relative error of at most 0.015.
Values may be sent and summed in bfloat16 or wider, within the bound.
A program may use at most 64 MiB of HBM per device.

v0:
```python
import jax
import jax.numpy as jnp
from jax import lax
from jax.sharding import PartitionSpec as P

S = 2048
F = 1024
LAGS = 256
BLOCK = 32
CH_DEV = 64


def forward_table():
    freq_index = jnp.arange(F, dtype=jnp.int32)
    time_index = jnp.arange(S, dtype=jnp.int32)
    phase = freq_index[:, None] * time_index[None, :] % S
    angles = phase.astype(jnp.float32) * (2.0 * jnp.pi / S)
    scale = 1.0 / jnp.sqrt(jnp.float32(S))
    return jnp.stack(
        [
            (jnp.cos(angles) * scale).astype(jnp.bfloat16),
            (-jnp.sin(angles) * scale).astype(jnp.bfloat16),
        ],
        axis=1,
    )


def lag_table():
    freq_index = jnp.arange(F, dtype=jnp.int32)
    shifts = (jnp.arange(LAGS, dtype=jnp.int32) - LAGS // 2) % S
    phase = freq_index[:, None] * shifts[None, :] % S
    angles = phase.astype(jnp.float32) * (2.0 * jnp.pi / S)
    scale = 1.0 / jnp.sqrt(jnp.float32(F))
    return jnp.stack(
        [
            (jnp.cos(angles) * scale).astype(jnp.bfloat16),
            (-jnp.sin(angles) * scale).astype(jnp.bfloat16),
        ],
        axis=1,
    )


def synthesize(incoming, table):
    count = incoming.shape[-1]
    flat = incoming.reshape(2 * F, count)
    result = jnp.einsum(
        "qn,qt->tn", flat, table.reshape(2 * F, S), preferred_element_type=jnp.float32
    )
    return result.astype(jnp.bfloat16)


def on_device(records, pairs, observed, lag_mask):
    fibre_count = lax.axis_size("fibre")
    seg_count = lax.axis_size("seg")
    spread_count = fibre_count * seg_count
    freq_dev = F // spread_count
    blocks_dev = CH_DEV // BLOCK
    block_count = CH_DEV * spread_count // BLOCK
    pair_total = pairs.shape[0]
    pairs_dev = pair_total // spread_count
    table = forward_table()
    lags = lag_table()
    spans = records.reshape(1, S // fibre_count, fibre_count, CH_DEV)
    incoming = lax.all_to_all(spans, "fibre", split_axis=2, concat_axis=1, tiled=True)
    count = incoming.shape[3]
    signal = incoming.reshape(S, count)
    result = jnp.einsum(
        "qs,sn->qn", table.reshape(2 * F, S), signal, preferred_element_type=jnp.float32
    )
    spectra = result.reshape(F, 2, count).astype(jnp.bfloat16)
    widened = lax.all_to_all(spectra, ("fibre", "seg"), split_axis=0, concat_axis=2, tiled=True)
    seg_blocks = fibre_count * blocks_dev
    slot_ids = (
        pairs % seg_blocks // blocks_dev * seg_count + pairs // seg_blocks
    ) * blocks_dev + pairs % blocks_dev
    blocks_grid = widened.reshape(freq_dev, 2, block_count, BLOCK)
    first_side = jnp.take(blocks_grid, slot_ids[:, 0], axis=2).astype(jnp.float32)
    second_side = jnp.take(blocks_grid, slot_ids[:, 1], axis=2).astype(jnp.float32)
    first_re, first_im = (first_side[:, 0], first_side[:, 1])
    second_re, second_im = (second_side[:, 0], second_side[:, 1])
    cross_re = first_re * second_re + first_im * second_im
    cross_im = first_im * second_re - first_re * second_im
    cross_spec = jnp.stack([cross_re, cross_im], axis=1).astype(jnp.bfloat16)
    cross_spec = cross_spec.reshape(freq_dev, 2, spread_count, pairs_dev * BLOCK)
    owned_spec = lax.all_to_all(
        cross_spec, ("fibre", "seg"), split_axis=2, concat_axis=0, tiled=True
    )
    owned_spec = owned_spec.reshape(F, 2, pairs_dev * BLOCK)
    partial_corr = jnp.einsum("wpx,wpl->xl", owned_spec, lags, preferred_element_type=jnp.float32)
    synthetic = (
        lax.psum(partial_corr.astype(jnp.bfloat16), "rec")
        .astype(jnp.float32)
        .reshape(pairs_dev, BLOCK, LAGS)
    )
    weights = lag_mask[:, None, :].astype(jnp.float32) * jnp.tanh(synthetic - observed)
    weights_low = weights.astype(jnp.bfloat16).reshape(pairs_dev * BLOCK, LAGS)
    adjoint_spec = jnp.einsum("xl,wpl->wpx", weights_low, lags, preferred_element_type=jnp.float32)
    adjoint_spec = adjoint_spec.astype(jnp.bfloat16).reshape(F, 2, 1, pairs_dev * BLOCK)
    returned = lax.all_to_all(
        adjoint_spec, ("fibre", "seg"), split_axis=0, concat_axis=2, tiled=True
    )
    returned = returned.reshape(freq_dev, 2, pair_total, BLOCK).astype(jnp.float32)
    adjoint_re, adjoint_im = (returned[:, 0], returned[:, 1])
    grad_first = jnp.stack(
        [
            adjoint_re * second_re - adjoint_im * second_im,
            adjoint_re * second_im + adjoint_im * second_re,
        ],
        axis=1,
    )
    grad_second = jnp.stack(
        [
            adjoint_re * first_re + adjoint_im * first_im,
            adjoint_re * first_im - adjoint_im * first_re,
        ],
        axis=1,
    )
    contributions = jnp.concatenate([grad_first, grad_second], axis=2)
    endpoint_ids = jnp.concatenate([slot_ids[:, 0], slot_ids[:, 1]])
    summed = jax.ops.segment_sum(
        jnp.moveaxis(contributions, 2, 0), endpoint_ids, num_segments=block_count
    )
    block_adjoint = jnp.moveaxis(summed, 0, 2).astype(jnp.bfloat16)
    outgoing = block_adjoint.reshape(freq_dev, 2, spread_count, CH_DEV)
    sources = synthesize(
        lax.all_to_all(outgoing, ("fibre", "seg"), split_axis=2, concat_axis=0, tiled=True), table
    )
    regrouped = lax.all_to_all(sources, "fibre", split_axis=0, concat_axis=1, tiled=True)
    return regrouped[None]


def solution(mesh):
    in_specs = (
        P("rec", "fibre", ("groups", "seg")),
        P(),
        P(("groups", "fibre", "seg"), None, None),
        P(("groups", "fibre", "seg"), None),
    )
    out_specs = P("rec", "fibre", ("groups", "seg"))
    return jax.shard_map(
        on_device, mesh=mesh, in_specs=in_specs, out_specs=out_specs, check_vma=False
    )
```

profile of v0, /device:TPU:0, one launch (start us, length us, event | category | flops | bytes accessed | tf_op | source)
XLA Modules:
  0.0 163.2 jit_solution(8597783628842389983)
XLA Ops:
  0.0 1.8 %copy.59 = bf16[1,512,256]{1,2,0:T(8,128)(2,1)} copy(bf16[1,512,256]{2,1,0:T(8,128)(2,1)} %param.6) | data formatting | bytes 524288 | tf_op args[0]
  1.8 6.3 %all-to-all-start = ((bf16[1,512,4,64]{1,3,0,2:T(8,128)(2,1)}), bf16[1,512,4,64]{1,3,0,2:T(8,128)(2,1)S(1)}, u32[]{:S(2)}, u32[]{:S(2)}) async-start(bf16[1,512,4,64]{1,3,0,2:T(8,128)(2,1)} %bitcast.3), calls=%async_computation | async-start | bytes 524288 | tf_op jit(solution)/shard_map/all_to_all | solution.py:64
  8.1 35.0 %multiply_convert_fusion = (bf16[1024,1,2048]{2,0,1:T(8,128)(2,1)}, bf16[1024,1,2048]{2,0,1:T(8,128)(2,1)}) fusion(), kind=kLoop, calls=%fused_computation.10 | loop fusion | flops 39845888 | bytes 8388608 | tf_op jit(solution)/shard_map/convert_element_type | solution.py:22
  43.6 5.1 %convolution_convert_fusion.1 = bf16[1024,2,64]{0,2,1:T(8,128)(2,1)S(1)} fusion(bf16[2048,64,1]{0,1,2:T(8,128)(2,1)S(1)} %reshape.311, bf16[1024,1,2048]{2,0,1:T(8,128)(2,1)} %get-tuple-element.24, bf16[1024,1,2048]{2,0,1:T(8,128)(2,1)} %get-tuple-element.25), kind=kOutput, calls=%fused_computation.19 | convolution fusion | flops 541196288 | bytes 8912896 | tf_op jit(solution)/shard_map/qs,sn->qn/dot_general | solution.py:67
  48.7 0.4 copy.62
  49.1 1.1 reshape.316
  50.2 6.0 %all-to-all-start.1 = ((bf16[8,2,8192]{2,1,0:T(2,128)(2,1)}), bf16[8,2,8192]{2,1,0:T(2,128)(2,1)S(1)}, u32[]{:S(2)}, u32[]{:S(2)}) async-start(bf16[8,2,8192]{2,1,0:T(2,128)(2,1)} %reshape.316), calls=%async_computation.1 | async-start | bytes 524288 | tf_op jit(solution)/shard_map/all_to_all | solution.py:71
  56.3 8.4 %all-to-all-done.1 = bf16[8,2,8192]{2,1,0:T(2,128)(2,1)S(1)} async-done(((bf16[8,2,8192]{2,1,0:T(2,128)(2,1)}), bf16[8,2,8192]{2,1,0:T(2,128)(2,1)S(1)}, u32[]{:S(2)}, u32[]{:S(2)}) %all-to-all-start.1) | async-done | bytes 262176 | tf_op jit(solution)/shard_map/all_to_all | solution.py:71
  65.1 0.4 copy.79
  65.5 0.6 gather_fusion.1
  66.1 0.6 gather_fusion
  67.0 0.7 pad_maximum_fusion.4
  67.8 3.4 %all-to-all-start.2 = ((bf16[128,2,8,64]{0,3,1,2:T(8,128)(2,1)}), bf16[128,2,8,64]{0,3,1,2:T(8,128)(2,1)S(1)}, u32[]{:S(2)}, u32[]{:S(2)}) async-start(bf16[128,2,8,64]{0,3,1,2:T(8,128)(2,1)} %pad_maximum_fusion.4), calls=%async_computation.2 | async-start | bytes 524288 | tf_op jit(solution)/shard_map/all_to_all | solution.py:85
  71.2 4.5 %multiply_convert_fusion.3 = (bf16[1024,1,256]{2,0,1:T(8,128)(2,1)S(1)}, bf16[1024,1,256]{2,0,1:T(8,128)(2,1)S(1)}) fusion(s32[256]{0:T(256)S(1)} %and_select_fusion), kind=kLoop, calls=%fused_computation.30 | loop fusion | flops 4980736 | bytes 1049600 | tf_op jit(solution)/shard_map/convert_element_type | solution.py:36
  75.7 4.0 %all-to-all-done.2 = bf16[128,2,8,64]{0,3,1,2:T(8,128)(2,1)S(1)} async-done(((bf16[128,2,8,64]{0,3,1,2:T(8,128)(2,1)}), bf16[128,2,8,64]{0,3,1,2:T(8,128)(2,1)S(1)}, u32[]{:S(2)}, u32[]{:S(2)}) %all-to-all-start.2) | async-done | bytes 262176 | tf_op jit(solution)/shard_map/all_to_all | solution.py:85
  80.3 3.4 %psum.7 = bf16[2,32,256]{2,1,0:T(8,128)(2,1)S(1)} all-reduce(bf16[2,32,256]{2,1,0:T(8,128)(2,1)S(1)} %bitcast.121), channel_id=1, replica_groups=mesh['groups'=2,'fibre'=4,'seg'=2,'rec'=2] {'rec'}, use_global_device_ids=true, to_apply=%region_0.2 | all-reduce | flops 16384 | bytes 65536 | tf_op jit(solution)/shard_map/psum | solution.py:91
  83.8 0.4 fusion.6
  84.2 0.4 copy.68
  84.6 1.1 reshape.318
  85.7 3.6 %all-to-all-start.3 = ((bf16[8,2,8192]{2,1,0:T(2,128)(2,1)}), bf16[8,2,8192]{2,1,0:T(2,128)(2,1)S(1)}, u32[]{:S(2)}, u32[]{:S(2)}) async-start(bf16[8,2,8192]{2,1,0:T(2,128)(2,1)} %reshape.318), calls=%async_computation.3 | async-start | bytes 524288 | tf_op jit(solution)/shard_map/all_to_all | solution.py:99
  89.3 9.4 %all-to-all-done.3 = bf16[8,2,8192]{2,1,0:T(2,128)(2,1)S(1)} async-done(((bf16[8,2,8192]{2,1,0:T(2,128)(2,1)}), bf16[8,2,8192]{2,1,0:T(2,128)(2,1)S(1)}, u32[]{:S(2)}, u32[]{:S(2)}) %all-to-all-start.3) | async-done | bytes 262176 | tf_op jit(solution)/shard_map/all_to_all | solution.py:99
  99.1 0.4 copy.69
  100.1 2.1 %scatter_fusion = f32[16,128,2,32]{1,3,2,0:T(8,128)S(1)} fusion(f32[16,128,2,32]{1,3,2,0:T(8,128)S(1)} %broadcast_in_dim.23, s32[32]{0:T(128)S(1)} %pad_add_fusion, f32[32,128,2,32]{1,3,2,0:T(8,128)S(1)} %maximum_bitcast_fusion), kind=kCustom, calls=%fused_computation.2 | custom fusion | flops 262144 | bytes 3145856 | tf_op jit(solution)/shard_map/scatter-add | solution.py:120
  102.3 0.7 copy.74
  103.1 3.6 %all-to-all-start.4 = ((bf16[128,2,8,64]{0,3,1,2:T(8,128)(2,1)}), bf16[128,2,8,64]{0,3,1,2:T(8,128)(2,1)S(1)}, u32[]{:S(2)}, u32[]{:S(2)}) async-start(bf16[128,2,8,64]{0,3,1,2:T(8,128)(2,1)} %copy.74), calls=%async_computation.4 | async-start | bytes 524288 | tf_op jit(solution)/shard_map/all_to_all | solution.py:126
  106.7 7.5 %pad_maximum_fusion = bf16[1024,2,2048]{2,0,1:T(8,128)(2,1)} fusion(bf16[1024,1,2048]{2,0,1:T(8,128)(2,1)} %get-tuple-element.24, bf16[1024,1,2048]{2,0,1:T(8,128)(2,1)} %get-tuple-element.25), kind=kLoop, calls=%fused_computation.9 | loop fusion | flops 4194304 | bytes 16777216 | tf_op jit(solution)/shard_map/stack | solution.py:19
  114.1 16.4 %copy.58 = bf16[1024,2,2048]{2,1,0:T(2,128)(2,1)} copy(bf16[1024,2,2048]{2,0,1:T(8,128)(2,1)} %pad_maximum_fusion) | data formatting | bytes 16777216 | tf_op jit(solution)/shard_map/stack | solution.py:19
  130.5 13.1 %reshape.267 = bf16[2048,2048]{1,0:T(8,128)(2,1)} reshape(bf16[1024,2,2048]{2,1,0:T(2,128)(2,1)} %copy.58) | data formatting | bytes 16777216 | tf_op jit(solution)/shard_map/reshape | solution.py:47
  143.6 0.4 copy.75
  144.0 5.0 %convolution_convert_fusion = bf16[2048,64]{0,1:T(8,128)(2,1)S(1)} fusion(bf16[2048,2048]{1,0:T(8,128)(2,1)} %reshape.267, bf16[2048,64]{1,0:T(8,128)(2,1)S(1)} %bitcast.106), kind=kOutput, calls=%fused_computation.15 | convolution fusion | flops 537001984 | bytes 8912896 | tf_op jit(solution)/shard_map/qn,qt->tn/dot_general | solution.py:46
  149.1 13.3 %all_to_all.85 = bf16[4,512,64]{1,2,0:T(8,128)(2,1)S(1)} all-to-all(bf16[4,512,64]{1,2,0:T(8,128)(2,1)S(1)} %bitcast.117), channel_id=1, replica_groups=mesh['groups'=2,'fibre'=4,'seg'=2,'rec'=2] {'fibre'}, dimensions={0} | all-to-all | bytes 524288 | tf_op jit(solution)/shard_map/all_to_all | solution.py:128
  162.3 0.8 copy.77
  (35 shorter events, 2.8 us)
Async XLA Ops:
  1.8 41.4 %all-to-all-start = ((bf16[1,512,4,64]{1,3,0,2:T(8,128)(2,1)}), bf16[1,512,4,64]{1,3,0,2:T(8,128)(2,1)S(1)}, u32[]{:S(2)}, u32[]{:S(2)}) async-start(bf16[1,512,4,64]{1,3,0,2:T(8,128)(2,1)} %bitcast.3), calls=%async_computation | async-start | bytes 524288 | tf_op jit(solution)/shard_map/all_to_all | solution.py:64
  43.6 12.6 %copy-start.2 = (s32[16,2]{0,1:T(2,128)S(1)}, s32[16,2]{0,1:T(2,128)}, u32[]{:S(2)}) copy-start(s32[16,2]{0,1:T(2,128)} %param.7) | copy-start | bytes 388
  48.7 22.5 %copy-start.1 = (s32[2,256]{1,0:T(2,128)S(1)}, s32[2,256]{1,0:T(2,128)}, u32[]{:S(2)}) copy-start(s32[2,256]{1,0:T(2,128)} %param.9) | copy-start | bytes 6148
  48.7 35.0 %copy-start = (f32[2,32,256]{2,1,0:T(8,128)S(1)}, f32[2,32,256]{2,1,0:T(8,128)}, u32[]{:S(2)}) copy-start(f32[2,32,256]{2,1,0:T(8,128)} %param.8) | copy-start | bytes 196612
  50.2 14.5 %all-to-all-start.1 = ((bf16[8,2,8192]{2,1,0:T(2,128)(2,1)}), bf16[8,2,8192]{2,1,0:T(2,128)(2,1)S(1)}, u32[]{:S(2)}, u32[]{:S(2)}) async-start(bf16[8,2,8192]{2,1,0:T(2,128)(2,1)} %reshape.316), calls=%async_computation.1 | async-start | bytes 524288 | tf_op jit(solution)/shard_map/all_to_all | solution.py:71
  67.8 12.0 %all-to-all-start.2 = ((bf16[128,2,8,64]{0,3,1,2:T(8,128)(2,1)}), bf16[128,2,8,64]{0,3,1,2:T(8,128)(2,1)S(1)}, u32[]{:S(2)}, u32[]{:S(2)}) async-start(bf16[128,2,8,64]{0,3,1,2:T(8,128)(2,1)} %pad_maximum_fusion.4), calls=%async_computation.2 | async-start | bytes 524288 | tf_op jit(solution)/shard_map/all_to_all | solution.py:85
  85.7 13.1 %all-to-all-start.3 = ((bf16[8,2,8192]{2,1,0:T(2,128)(2,1)}), bf16[8,2,8192]{2,1,0:T(2,128)(2,1)S(1)}, u32[]{:S(2)}, u32[]{:S(2)}) async-start(bf16[8,2,8192]{2,1,0:T(2,128)(2,1)} %reshape.318), calls=%async_computation.3 | async-start | bytes 524288 | tf_op jit(solution)/shard_map/all_to_all | solution.py:99
  103.1 40.6 %all-to-all-start.4 = ((bf16[128,2,8,64]{0,3,1,2:T(8,128)(2,1)}), bf16[128,2,8,64]{0,3,1,2:T(8,128)(2,1)S(1)}, u32[]{:S(2)}, u32[]{:S(2)}) async-start(bf16[128,2,8,64]{0,3,1,2:T(8,128)(2,1)} %copy.74), calls=%async_computation.4 | async-start | bytes 524288 | tf_op jit(solution)/shard_map/all_to_all | solution.py:126
where the time goes:
time: 164 us; the launch traced here: 163 us
  other arithmetic  50.7 us (31%)
  local copies, waits for them, and re-layouts  39.9 us (24%)
  starting transfers between devices  23 us (14%)
  waiting for transfers between devices  21.9 us (13%)
  blocking collectives  16.7 us (10%)
  matrix products  10.8 us (7%)
    convert_element_type x1, other arithmetic, forward_table(): (-jnp.sin(angles) * scale).astype(jnp.bfloat16)  35 us
    another operation x1, local copies, waits for them, and re-layouts, forward_table(): jnp.stack([(jnp.cos(angles) * scale).astype(jnp.bfloat16), (-jnp.sin(angl...  16.4 us
    all_to_all x1, blocking collectives, on_device(): lax.all_to_all(sources, 'fibre', split_axis=0, concat_axis=1, tiled=True)  13.3 us
    reshape x1, local copies, waits for them, and re-layouts, synthesize(): table.reshape(2 * F, S)  13.1 us
    all_to_all x1, waiting for transfers between devices, on_device(): lax.all_to_all(adjoint_spec, ('fibre', 'seg'), split_axis=0, concat_axis=...  9.42 us
    all_to_all x1, waiting for transfers between devices, on_device(): lax.all_to_all(spectra, ('fibre', 'seg'), split_axis=0, concat_axis=2, ti...  8.44 us
    another operation x1, other arithmetic, forward_table(): jnp.stack([(jnp.cos(angles) * scale).astype(jnp.bfloat16), (-jnp.sin(angl...  7.45 us
    all_to_all x1, starting transfers between devices, on_device(): lax.all_to_all(spans, 'fibre', split_axis=2, concat_axis=1, tiled=True)  6.35 us
  transfers between devices with their start and end apart: 5, of which 3 were waited for; matrix products, arithmetic and copies ran while one was open for 47% of the time, Pallas kernels for 0%

commit v1 on v0

--- a/solution.py
+++ b/solution.py
@@ -125,7 +125,12 @@
     sources = synthesize(
         lax.all_to_all(outgoing, ("fibre", "seg"), split_axis=2, concat_axis=0, tiled=True), table
     )
-    regrouped = lax.all_to_all(sources, "fibre", split_axis=0, concat_axis=1, tiled=True)
+    regrouped = jnp.concatenate(
+        lax.all_to_all(
+            jnp.stack(jnp.split(sources, lax.axis_size("fibre"), axis=0)), "fibre", 0, 0
+        ),
+        axis=1,
+    )
     return regrouped[None]
 
 

time: 164 us -> 164 us (level)
  no operation moved by 1% of the time
where the time goes in v1:
time: 164 us; the launch traced here: 163 us
  other arithmetic  50.7 us (31%)
  local copies, waits for them, and re-layouts  39.9 us (24%)
  starting transfers between devices  23 us (14%)
  waiting for transfers between devices  21.9 us (13%)
  blocking collectives  16.7 us (10%)
  matrix products  10.8 us (7%)
    convert_element_type x1, other arithmetic, forward_table(): (-jnp.sin(angles) * scale).astype(jnp.bfloat16)  35 us
    another operation x1, local copies, waits for them, and re-layouts, forward_table(): jnp.stack([(jnp.cos(angles) * scale).astype(jnp.bfloat16), (-jnp.sin(angl...  16.4 us
    all_to_all x1, blocking collectives, on_device(): lax.all_to_all(jnp.stack(jnp.split(sources, lax.axis_size('fibre'), axis=...  13.3 us
    reshape x1, local copies, waits for them, and re-layouts, synthesize(): table.reshape(2 * F, S)  13.1 us
    all_to_all x1, waiting for transfers between devices, on_device(): lax.all_to_all(adjoint_spec, ('fibre', 'seg'), split_axis=0, concat_axis=...  9.42 us
    all_to_all x1, waiting for transfers between devices, on_device(): lax.all_to_all(spectra, ('fibre', 'seg'), split_axis=0, concat_axis=2, ti...  8.44 us
    another operation x1, other arithmetic, forward_table(): jnp.stack([(jnp.cos(angles) * scale).astype(jnp.bfloat16), (-jnp.sin(angl...  7.45 us
    all_to_all x1, starting transfers between devices, on_device(): lax.all_to_all(spans, 'fibre', split_axis=2, concat_axis=1, tiled=True)  6.35 us
  transfers between devices with their start and end apart: 5, of which 3 were waited for; matrix products, arithmetic and copies ran while one was open for 47% of the time, Pallas kernels for 0%

profile of v1, /device:TPU:0, one launch (start us, length us, event | category | flops | bytes accessed | tf_op | source)
XLA Modules:
  0.0 163.2 jit_solution(5779909836414437357)
XLA Ops:
  0.0 1.8 %copy.56 = bf16[1,512,256]{1,2,0:T(8,128)(2,1)} copy(bf16[1,512,256]{2,1,0:T(8,128)(2,1)} %param.6) | data formatting | bytes 524288 | tf_op args[0]
  1.8 6.3 %all-to-all-start = ((bf16[1,512,4,64]{1,3,0,2:T(8,128)(2,1)}), bf16[1,512,4,64]{1,3,0,2:T(8,128)(2,1)S(1)}, u32[]{:S(2)}, u32[]{:S(2)}) async-start(bf16[1,512,4,64]{1,3,0,2:T(8,128)(2,1)} %bitcast.3), calls=%async_computation | async-start | bytes 524288 | tf_op jit(solution)/shard_map/all_to_all | solution.py:64
  8.1 35.0 %multiply_convert_fusion = (bf16[1024,1,2048]{2,0,1:T(8,128)(2,1)}, bf16[1024,1,2048]{2,0,1:T(8,128)(2,1)}) fusion(), kind=kLoop, calls=%fused_computation.10 | loop fusion | flops 39845888 | bytes 8388608 | tf_op jit(solution)/shard_map/convert_element_type | solution.py:22
  43.6 5.1 %convolution_convert_fusion.1 = bf16[1024,2,64]{0,2,1:T(8,128)(2,1)S(1)} fusion(bf16[2048,64,1]{0,1,2:T(8,128)(2,1)S(1)} %reshape.311, bf16[1024,1,2048]{2,0,1:T(8,128)(2,1)} %get-tuple-element.28, bf16[1024,1,2048]{2,0,1:T(8,128)(2,1)} %get-tuple-element.29), kind=kOutput, calls=%fused_computation.19 | convolution fusion | flops 541196288 | bytes 8912896 | tf_op jit(solution)/shard_map/qs,sn->qn/dot_general | solution.py:67
  48.7 0.4 copy.59
  49.1 1.1 reshape.316
  50.2 6.0 %all-to-all-start.1 = ((bf16[8,2,8192]{2,1,0:T(2,128)(2,1)}), bf16[8,2,8192]{2,1,0:T(2,128)(2,1)S(1)}, u32[]{:S(2)}, u32[]{:S(2)}) async-start(bf16[8,2,8192]{2,1,0:T(2,128)(2,1)} %reshape.316), calls=%async_computation.1 | async-start | bytes 524288 | tf_op jit(solution)/shard_map/all_to_all | solution.py:71
  56.3 8.4 %all-to-all-done.1 = bf16[8,2,8192]{2,1,0:T(2,128)(2,1)S(1)} async-done(((bf16[8,2,8192]{2,1,0:T(2,128)(2,1)}), bf16[8,2,8192]{2,1,0:T(2,128)(2,1)S(1)}, u32[]{:S(2)}, u32[]{:S(2)}) %all-to-all-start.1) | async-done | bytes 262176 | tf_op jit(solution)/shard_map/all_to_all | solution.py:71
  65.1 0.4 copy.75
  65.5 0.6 gather_fusion.1
  66.1 0.6 gather_fusion
  67.0 0.7 pad_maximum_fusion.4
  67.8 3.4 %all-to-all-start.2 = ((bf16[128,2,8,64]{0,3,1,2:T(8,128)(2,1)}), bf16[128,2,8,64]{0,3,1,2:T(8,128)(2,1)S(1)}, u32[]{:S(2)}, u32[]{:S(2)}) async-start(bf16[128,2,8,64]{0,3,1,2:T(8,128)(2,1)} %pad_maximum_fusion.4), calls=%async_computation.2 | async-start | bytes 524288 | tf_op jit(solution)/shard_map/all_to_all | solution.py:85
  71.2 4.5 %multiply_convert_fusion.3 = (bf16[1024,1,256]{2,0,1:T(8,128)(2,1)S(1)}, bf16[1024,1,256]{2,0,1:T(8,128)(2,1)S(1)}) fusion(s32[256]{0:T(256)S(1)} %and_select_fusion), kind=kLoop, calls=%fused_computation.30 | loop fusion | flops 4980736 | bytes 1049600 | tf_op jit(solution)/shard_map/convert_element_type | solution.py:36
  75.7 4.0 %all-to-all-done.2 = bf16[128,2,8,64]{0,3,1,2:T(8,128)(2,1)S(1)} async-done(((bf16[128,2,8,64]{0,3,1,2:T(8,128)(2,1)}), bf16[128,2,8,64]{0,3,1,2:T(8,128)(2,1)S(1)}, u32[]{:S(2)}, u32[]{:S(2)}) %all-to-all-start.2) | async-done | bytes 262176 | tf_op jit(solution)/shard_map/all_to_all | solution.py:85
  80.3 3.4 %psum.7 = bf16[2,32,256]{2,1,0:T(8,128)(2,1)S(1)} all-reduce(bf16[2,32,256]{2,1,0:T(8,128)(2,1)S(1)} %bitcast.123), channel_id=1, replica_groups=mesh['groups'=2,'fibre'=4,'seg'=2,'rec'=2] {'rec'}, use_global_device_ids=true, to_apply=%region_0.2 | all-reduce | flops 16384 | bytes 65536 | tf_op jit(solution)/shard_map/psum | solution.py:91
  83.8 0.4 fusion.6
  84.2 0.4 copy.65
  84.6 1.1 reshape.318
  85.7 3.6 %all-to-all-start.3 = ((bf16[8,2,8192]{2,1,0:T(2,128)(2,1)}), bf16[8,2,8192]{2,1,0:T(2,128)(2,1)S(1)}, u32[]{:S(2)}, u32[]{:S(2)}) async-start(bf16[8,2,8192]{2,1,0:T(2,128)(2,1)} %reshape.318), calls=%async_computation.3 | async-start | bytes 524288 | tf_op jit(solution)/shard_map/all_to_all | solution.py:99
  89.3 9.4 %all-to-all-done.3 = bf16[8,2,8192]{2,1,0:T(2,128)(2,1)S(1)} async-done(((bf16[8,2,8192]{2,1,0:T(2,128)(2,1)}), bf16[8,2,8192]{2,1,0:T(2,128)(2,1)S(1)}, u32[]{:S(2)}, u32[]{:S(2)}) %all-to-all-start.3) | async-done | bytes 262176 | tf_op jit(solution)/shard_map/all_to_all | solution.py:99
  99.1 0.4 copy.66
  100.1 2.1 %scatter_fusion = f32[16,128,2,32]{1,3,2,0:T(8,128)S(1)} fusion(f32[16,128,2,32]{1,3,2,0:T(8,128)S(1)} %broadcast_in_dim.20, s32[32]{0:T(128)S(1)} %pad_add_fusion, f32[32,128,2,32]{1,3,2,0:T(8,128)S(1)} %maximum_bitcast_fusion), kind=kCustom, calls=%fused_computation.2 | custom fusion | flops 262144 | bytes 3145856 | tf_op jit(solution)/shard_map/scatter-add | solution.py:120
  102.3 0.7 copy.71
  103.1 3.6 %all-to-all-start.4 = ((bf16[128,2,8,64]{0,3,1,2:T(8,128)(2,1)}), bf16[128,2,8,64]{0,3,1,2:T(8,128)(2,1)S(1)}, u32[]{:S(2)}, u32[]{:S(2)}) async-start(bf16[128,2,8,64]{0,3,1,2:T(8,128)(2,1)} %copy.71), calls=%async_computation.4 | async-start | bytes 524288 | tf_op jit(solution)/shard_map/all_to_all | solution.py:126
  106.7 7.4 %pad_maximum_fusion = bf16[1024,2,2048]{2,0,1:T(8,128)(2,1)} fusion(bf16[1024,1,2048]{2,0,1:T(8,128)(2,1)} %get-tuple-element.28, bf16[1024,1,2048]{2,0,1:T(8,128)(2,1)} %get-tuple-element.29), kind=kLoop, calls=%fused_computation.9 | loop fusion | flops 4194304 | bytes 16777216 | tf_op jit(solution)/shard_map/stack | solution.py:19
  114.1 16.4 %copy.55 = bf16[1024,2,2048]{2,1,0:T(2,128)(2,1)} copy(bf16[1024,2,2048]{2,0,1:T(8,128)(2,1)} %pad_maximum_fusion) | data formatting | bytes 16777216 | tf_op jit(solution)/shard_map/stack | solution.py:19
  130.5 13.1 %reshape.266 = bf16[2048,2048]{1,0:T(8,128)(2,1)} reshape(bf16[1024,2,2048]{2,1,0:T(2,128)(2,1)} %copy.55) | data formatting | bytes 16777216 | tf_op jit(solution)/shard_map/reshape | solution.py:47
  143.7 0.4 copy.72
  144.1 5.0 %convolution_convert_fusion = bf16[2048,64]{0,1:T(8,128)(2,1)S(1)} fusion(bf16[2048,2048]{1,0:T(8,128)(2,1)} %reshape.266, bf16[2048,64]{1,0:T(8,128)(2,1)S(1)} %bitcast.110), kind=kOutput, calls=%fused_computation.15 | convolution fusion | flops 537001984 | bytes 8912896 | tf_op jit(solution)/shard_map/qn,qt->tn/dot_general | solution.py:46
  149.1 13.3 %all_to_all.74 = bf16[4,512,64]{1,2,0:T(8,128)(2,1)S(1)} all-to-all(bf16[4,512,64]{1,2,0:T(8,128)(2,1)S(1)} %pad_maximum_fusion.5), channel_id=1, replica_groups=mesh['groups'=2,'fibre'=4,'seg'=2,'rec'=2] {'fibre'}, dimensions={0} | all-to-all | bytes 524288 | tf_op jit(solution)/shard_map/all_to_all | solution.py:129
  162.4 0.8 copy.73
  (36 shorter events, 2.8 us)
Async XLA Ops:
  1.8 41.4 %all-to-all-start = ((bf16[1,512,4,64]{1,3,0,2:T(8,128)(2,1)}), bf16[1,512,4,64]{1,3,0,2:T(8,128)(2,1)S(1)}, u32[]{:S(2)}, u32[]{:S(2)}) async-start(bf16[1,512,4,64]{1,3,0,2:T(8,128)(2,1)} %bitcast.3), calls=%async_computation | async-start | bytes 524288 | tf_op jit(solution)/shard_map/all_to_all | solution.py:64
  43.6 12.6 %copy-start.2 = (s32[16,2]{0,1:T(2,128)S(1)}, s32[16,2]{0,1:T(2,128)}, u32[]{:S(2)}) copy-start(s32[16,2]{0,1:T(2,128)} %param.7) | copy-start | bytes 388
  48.7 22.5 %copy-start.1 = (s32[2,256]{1,0:T(2,128)S(1)}, s32[2,256]{1,0:T(2,128)}, u32[]{:S(2)}) copy-start(s32[2,256]{1,0:T(2,128)} %param.9) | copy-start | bytes 6148
  48.7 35.0 %copy-start = (f32[2,32,256]{2,1,0:T(8,128)S(1)}, f32[2,32,256]{2,1,0:T(8,128)}, u32[]{:S(2)}) copy-start(f32[2,32,256]{2,1,0:T(8,128)} %param.8) | copy-start | bytes 196612
  50.2 14.5 %all-to-all-start.1 = ((bf16[8,2,8192]{2,1,0:T(2,128)(2,1)}), bf16[8,2,8192]{2,1,0:T(2,128)(2,1)S(1)}, u32[]{:S(2)}, u32[]{:S(2)}) async-start(bf16[8,2,8192]{2,1,0:T(2,128)(2,1)} %reshape.316), calls=%async_computation.1 | async-start | bytes 524288 | tf_op jit(solution)/shard_map/all_to_all | solution.py:71
  67.8 12.0 %all-to-all-start.2 = ((bf16[128,2,8,64]{0,3,1,2:T(8,128)(2,1)}), bf16[128,2,8,64]{0,3,1,2:T(8,128)(2,1)S(1)}, u32[]{:S(2)}, u32[]{:S(2)}) async-start(bf16[128,2,8,64]{0,3,1,2:T(8,128)(2,1)} %pad_maximum_fusion.4), calls=%async_computation.2 | async-start | bytes 524288 | tf_op jit(solution)/shard_map/all_to_all | solution.py:85
  85.7 13.1 %all-to-all-start.3 = ((bf16[8,2,8192]{2,1,0:T(2,128)(2,1)}), bf16[8,2,8192]{2,1,0:T(2,128)(2,1)S(1)}, u32[]{:S(2)}, u32[]{:S(2)}) async-start(bf16[8,2,8192]{2,1,0:T(2,128)(2,1)} %reshape.318), calls=%async_computation.3 | async-start | bytes 524288 | tf_op jit(solution)/shard_map/all_to_all | solution.py:99
  103.1 40.6 %all-to-all-start.4 = ((bf16[128,2,8,64]{0,3,1,2:T(8,128)(2,1)}), bf16[128,2,8,64]{0,3,1,2:T(8,128)(2,1)S(1)}, u32[]{:S(2)}, u32[]{:S(2)}) async-start(bf16[128,2,8,64]{0,3,1,2:T(8,128)(2,1)} %copy.71), calls=%async_computation.4 | async-start | bytes 524288 | tf_op jit(solution)/shard_map/all_to_all | solution.py:126
